TPU v7x, 32 devices: a whole 2x2x4 slice. The times are simulated.
32 devices in a mesh: data: 2 (over x), seq: 4 (over z), dap: 4 (over y, core).
Axes of the slice: x: 2, y: 2, z: 4, core: 2. Of those that a mesh axis runs over, the one named last changes fastest.
Arguments:
- msa_act: bfloat16 [2048, 384, 256], P(('data', 'seq'), 'dap'), parts along dimension 0
- msa_mask: int32 [2048, 384], P('data'), parts along dimension 0
- pair_act: float32 [768, 384, 128], P(('data', 'dap')), parts along dimension 0
- ln_gamma: bfloat16 [256], replicated
- ln_beta: bfloat16 [256], replicated
- w_left: bfloat16 [256, 32], replicated
- b_left: bfloat16 [32], replicated
- w_right: bfloat16 [256, 32], replicated
- b_right: bfloat16 [32], replicated
- w_out: bfloat16 [1024, 128], replicated
- b_out: bfloat16 [128], replicated
Outputs:
- output 1: float32 [768, 384, 128], P(('data', 'dap')), parts along dimension 0
- output 2: bfloat16 [2048, 384, 256], P(('data', 'seq', 'dap')), parts along dimension 0
There are 2 independent parts. A program takes and returns all parts, laid end to end along the dimension named above; an argument that names none is the same for every part.
All inputs are finite; a program needn't handle non-finite values.
Results may differ from a plain program's by a relative error of at most 0.0107188.
Values are sent between devices in bfloat16 or wider.
A program may use at most 1 GiB of HBM per device.

v0:
```python
import jax
import jax.numpy as jnp
from jax import lax
from jax.sharding import PartitionSpec as P


def block_rows(rows_total, row_width):
    target = max(1, 16384 // row_width)
    return max(divisor for divisor in range(1, min(rows_total, target) + 1) if rows_total % divisor == 0)


def layer_norm(value_a7, ln_gamma, ln_beta):
    act_f32 = value_a7.astype(jnp.float32)
    mean_val = jnp.mean(act_f32, axis=-1, keepdims=True)
    centered = act_f32 - mean_val
    var_val = jnp.mean(centered * centered, axis=-1, keepdims=True)
    normed = centered * lax.rsqrt(var_val + 1e-5)
    return (normed * ln_gamma.astype(jnp.float32) + ln_beta.astype(jnp.float32)).astype(jnp.bfloat16)


def project(normed, weight, bias_vec, mask_f32):
    flat_act = normed.reshape(-1, normed.shape[-1])
    out_f32 = jnp.dot(flat_act, weight, preferred_element_type=jnp.float32) + bias_vec.astype(jnp.float32)
    return (out_f32.reshape(normed.shape[:-1] + (weight.shape[1],)) * mask_f32[:, :, None]).astype(jnp.bfloat16)


def pair_partial(left_proj, right_proj, w_out3):
    n_seq = left_proj.shape[0]
    n_rows = left_proj.shape[1]
    c_hid = left_proj.shape[2]
    n_cols = right_proj.shape[1]
    rows_per = block_rows(n_rows, n_cols)
    left_blocks = jnp.moveaxis(left_proj.reshape(n_seq, n_rows // rows_per, rows_per, c_hid), 1, 0)

    def one_block(left_blk):
        outer_blk = jnp.einsum('sic,sjd->icjd', left_blk, right_proj, preferred_element_type=jnp.float32).astype(jnp.bfloat16)
        return jnp.einsum('icjd,cde->ije', outer_blk, w_out3, preferred_element_type=jnp.float32).astype(jnp.bfloat16)

    return lax.map(one_block, left_blocks).reshape(n_rows, n_cols, w_out3.shape[2])


def solution(mesh):
    dap_size = mesh.shape['dap']
    replicated = P()
    in_specs = (P(('data', 'seq'), 'dap', None), P('data', None), P(('data', 'dap'), None, None), replicated, replicated, replicated, replicated, replicated, replicated, replicated, replicated)
    out_specs = (P(('data', 'dap'), None, None), P(('data', 'seq', 'dap'), None, None))

    def local_fn(array_b7, mask_part, pair_rows, ln_gamma, ln_beta, w_left, b_left, w_right, b_right, w_out, b_out):
        seq_idx = lax.axis_index('seq')
        dap_idx = lax.axis_index('dap')
        local_c7 = lax.all_to_all(array_b7, 'dap', 0, 1, tiled=True)
        n_local = local_c7.shape[0]
        n_rows = pair_rows.shape[0]
        c_hid = w_left.shape[1]
        mask_seq = lax.dynamic_slice_in_dim(mask_part, (seq_idx * dap_size + dap_idx) * n_local, n_local, axis=0).astype(jnp.float32)
        normed = layer_norm(local_c7, ln_gamma, ln_beta)
        left_proj = project(normed, w_left, b_left, mask_seq)
        right_proj = project(normed, w_right, b_right, mask_seq)
        w_out3 = w_out.reshape(c_hid, c_hid, w_out.shape[1])
        partial = pair_partial(left_proj, right_proj, w_out3)
        summed = lax.psum_scatter(partial, 'dap', scatter_dimension=0, tiled=True)
        summed = lax.psum(summed, 'seq')
        mask_bf16 = mask_part.astype(jnp.bfloat16)
        mask_rows = lax.dynamic_slice_in_dim(mask_bf16, dap_idx * n_rows, n_rows, axis=1)
        pair_count = jnp.einsum('si,sj->ij', mask_rows, mask_bf16, preferred_element_type=jnp.float32)
        update = (summed.astype(jnp.float32) + b_out.astype(jnp.float32)) / (1e-3 + pair_count)[:, :, None]
        return pair_rows + update, local_c7

    return jax.shard_map(local_fn, mesh=mesh, in_specs=in_specs, out_specs=out_specs, check_vma=False)
```

profile of v0, /device:TPU:0, one launch (start us, length us, event | category | flops | bytes accessed | tf_op | source)
XLA Modules:
  0.0 1370.0 jit_solution(14798949476473147741)
XLA Ops:
  15.3 136.9 %all-to-all-done = bf16[256,96,256]{2,1,0:T(8,128)(2,1)} async-done(((bf16[256,96,256]{2,1,0:T(8,128)(2,1)}), bf16[256,96,256]{2,1,0:T(8,128)(2,1)}, u32[]{:S(2)}, u32[]{:S(2)}) %all-to-all-start) | async-done | bytes 12582944 | tf_op jit(solution)/shard_map/all_to_all | solution.py:51
  170.9 12.1 fusion.14
  183.0 13.3 fusion.9
  225.4 12.8 copy.22
  263.4 496.5 %while.10 = (s32[]{:T(128)}, bf16[12,32,384,128]{3,2,1,0:T(8,128)(2,1)}, bf16[12,64,32,32]{3,2,1,0:T(8,128)(2,1)}, bf16[64,384,32]{2,1,0:T(8,128)(2,1)}, bf16[32,32,128]{2,1,0:T(8,128)(2,1)S(1)}, /*index=5*/s32[]{:T(128)}) while((s32[]{:T(128)}, bf16[12,32,384,128]{3,2,1,0:T(8,128)(2,1)}, bf16[12,64,32,32]{3,2,1,0:T(8,128)(2,1)}, ...), condition=%wide.region_3.4_spmd, body=%wide.region_2.3_spmd.sunk | while | flops 4833411072 | bytes 58851912 | solution.py:39
  270.4 11.7 fusion.30
  282.2 22.6 %fusion.31 = bf16[12,32,384,128]{3,2,1,0:T(8,128)(2,1)} fusion(bf16[12,32,384,128]{3,2,1,0:T(8,128)(2,1)} %get-tuple-element.85, s32[]{:T(128)} %get-tuple-element.84, bf16[32,32,384,32]{2,1,3,0:T(8,128)(2,1)} %fusion.30, bf16[32,32,128]{2,1,0:T(8,128)(2,1)S(1)} %get-tuple-element.94), kind=kOutput, calls=%fused_computation.4.clone.1 | convolution fusion | flops 3222798336 | bytes 28574208 | tf_op jit(solution)/shard_map/while/body/eval_jaxpr/icjd,cde->ije/dot_general | solution.py:37
  311.8 11.7 fusion.30
  323.5 22.6 %fusion.31 = bf16[12,32,384,128]{3,2,1,0:T(8,128)(2,1)} fusion(bf16[12,32,384,128]{3,2,1,0:T(8,128)(2,1)} %get-tuple-element.85, s32[]{:T(128)} %get-tuple-element.84, bf16[32,32,384,32]{2,1,3,0:T(8,128)(2,1)} %fusion.30, bf16[32,32,128]{2,1,0:T(8,128)(2,1)S(1)} %get-tuple-element.94), kind=kOutput, calls=%fused_computation.4.clone.1 | convolution fusion | flops 3222798336 | bytes 28574208 | tf_op jit(solution)/shard_map/while/body/eval_jaxpr/icjd,cde->ije/dot_general | solution.py:37
  353.1 11.7 fusion.30
  364.9 22.7 %fusion.31 = bf16[12,32,384,128]{3,2,1,0:T(8,128)(2,1)} fusion(bf16[12,32,384,128]{3,2,1,0:T(8,128)(2,1)} %get-tuple-element.85, s32[]{:T(128)} %get-tuple-element.84, bf16[32,32,384,32]{2,1,3,0:T(8,128)(2,1)} %fusion.30, bf16[32,32,128]{2,1,0:T(8,128)(2,1)S(1)} %get-tuple-element.94), kind=kOutput, calls=%fused_computation.4.clone.1 | convolution fusion | flops 3222798336 | bytes 28574208 | tf_op jit(solution)/shard_map/while/body/eval_jaxpr/icjd,cde->ije/dot_general | solution.py:37
  394.6 11.7 fusion.30
  406.3 22.6 %fusion.31 = bf16[12,32,384,128]{3,2,1,0:T(8,128)(2,1)} fusion(bf16[12,32,384,128]{3,2,1,0:T(8,128)(2,1)} %get-tuple-element.85, s32[]{:T(128)} %get-tuple-element.84, bf16[32,32,384,32]{2,1,3,0:T(8,128)(2,1)} %fusion.30, bf16[32,32,128]{2,1,0:T(8,128)(2,1)S(1)} %get-tuple-element.94), kind=kOutput, calls=%fused_computation.4.clone.1 | convolution fusion | flops 3222798336 | bytes 28574208 | tf_op jit(solution)/shard_map/while/body/eval_jaxpr/icjd,cde->ije/dot_general | solution.py:37
  436.0 11.7 fusion.30
  447.7 22.6 %fusion.31 = bf16[12,32,384,128]{3,2,1,0:T(8,128)(2,1)} fusion(bf16[12,32,384,128]{3,2,1,0:T(8,128)(2,1)} %get-tuple-element.85, s32[]{:T(128)} %get-tuple-element.84, bf16[32,32,384,32]{2,1,3,0:T(8,128)(2,1)} %fusion.30, bf16[32,32,128]{2,1,0:T(8,128)(2,1)S(1)} %get-tuple-element.94), kind=kOutput, calls=%fused_computation.4.clone.1 | convolution fusion | flops 3222798336 | bytes 28574208 | tf_op jit(solution)/shard_map/while/body/eval_jaxpr/icjd,cde->ije/dot_general | solution.py:37
  477.3 11.7 fusion.30
  489.1 22.6 %fusion.31 = bf16[12,32,384,128]{3,2,1,0:T(8,128)(2,1)} fusion(bf16[12,32,384,128]{3,2,1,0:T(8,128)(2,1)} %get-tuple-element.85, s32[]{:T(128)} %get-tuple-element.84, bf16[32,32,384,32]{2,1,3,0:T(8,128)(2,1)} %fusion.30, bf16[32,32,128]{2,1,0:T(8,128)(2,1)S(1)} %get-tuple-element.94), kind=kOutput, calls=%fused_computation.4.clone.1 | convolution fusion | flops 3222798336 | bytes 28574208 | tf_op jit(solution)/shard_map/while/body/eval_jaxpr/icjd,cde->ije/dot_general | solution.py:37
  518.7 11.7 fusion.30
  530.5 22.6 %fusion.31 = bf16[12,32,384,128]{3,2,1,0:T(8,128)(2,1)} fusion(bf16[12,32,384,128]{3,2,1,0:T(8,128)(2,1)} %get-tuple-element.85, s32[]{:T(128)} %get-tuple-element.84, bf16[32,32,384,32]{2,1,3,0:T(8,128)(2,1)} %fusion.30, bf16[32,32,128]{2,1,0:T(8,128)(2,1)S(1)} %get-tuple-element.94), kind=kOutput, calls=%fused_computation.4.clone.1 | convolution fusion | flops 3222798336 | bytes 28574208 | tf_op jit(solution)/shard_map/while/body/eval_jaxpr/icjd,cde->ije/dot_general | solution.py:37
  560.1 11.7 fusion.30
  571.8 22.6 %fusion.31 = bf16[12,32,384,128]{3,2,1,0:T(8,128)(2,1)} fusion(bf16[12,32,384,128]{3,2,1,0:T(8,128)(2,1)} %get-tuple-element.85, s32[]{:T(128)} %get-tuple-element.84, bf16[32,32,384,32]{2,1,3,0:T(8,128)(2,1)} %fusion.30, bf16[32,32,128]{2,1,0:T(8,128)(2,1)S(1)} %get-tuple-element.94), kind=kOutput, calls=%fused_computation.4.clone.1 | convolution fusion | flops 3222798336 | bytes 28574208 | tf_op jit(solution)/shard_map/while/body/eval_jaxpr/icjd,cde->ije/dot_general | solution.py:37
  601.5 11.7 fusion.30
  613.2 22.6 %fusion.31 = bf16[12,32,384,128]{3,2,1,0:T(8,128)(2,1)} fusion(bf16[12,32,384,128]{3,2,1,0:T(8,128)(2,1)} %get-tuple-element.85, s32[]{:T(128)} %get-tuple-element.84, bf16[32,32,384,32]{2,1,3,0:T(8,128)(2,1)} %fusion.30, bf16[32,32,128]{2,1,0:T(8,128)(2,1)S(1)} %get-tuple-element.94), kind=kOutput, calls=%fused_computation.4.clone.1 | convolution fusion | flops 3222798336 | bytes 28574208 | tf_op jit(solution)/shard_map/while/body/eval_jaxpr/icjd,cde->ije/dot_general | solution.py:37
  642.8 11.7 fusion.30
  654.5 22.6 %fusion.31 = bf16[12,32,384,128]{3,2,1,0:T(8,128)(2,1)} fusion(bf16[12,32,384,128]{3,2,1,0:T(8,128)(2,1)} %get-tuple-element.85, s32[]{:T(128)} %get-tuple-element.84, bf16[32,32,384,32]{2,1,3,0:T(8,128)(2,1)} %fusion.30, bf16[32,32,128]{2,1,0:T(8,128)(2,1)S(1)} %get-tuple-element.94), kind=kOutput, calls=%fused_computation.4.clone.1 | convolution fusion | flops 3222798336 | bytes 28574208 | tf_op jit(solution)/shard_map/while/body/eval_jaxpr/icjd,cde->ije/dot_general | solution.py:37
  684.1 11.7 fusion.30
  695.9 22.6 %fusion.31 = bf16[12,32,384,128]{3,2,1,0:T(8,128)(2,1)} fusion(bf16[12,32,384,128]{3,2,1,0:T(8,128)(2,1)} %get-tuple-element.85, s32[]{:T(128)} %get-tuple-element.84, bf16[32,32,384,32]{2,1,3,0:T(8,128)(2,1)} %fusion.30, bf16[32,32,128]{2,1,0:T(8,128)(2,1)S(1)} %get-tuple-element.94), kind=kOutput, calls=%fused_computation.4.clone.1 | convolution fusion | flops 3222798336 | bytes 28574208 | tf_op jit(solution)/shard_map/while/body/eval_jaxpr/icjd,cde->ije/dot_general | solution.py:37
  725.5 11.7 fusion.30
  737.2 22.7 %fusion.31 = bf16[12,32,384,128]{3,2,1,0:T(8,128)(2,1)} fusion(bf16[12,32,384,128]{3,2,1,0:T(8,128)(2,1)} %get-tuple-element.85, s32[]{:T(128)} %get-tuple-element.84, bf16[32,32,384,32]{2,1,3,0:T(8,128)(2,1)} %fusion.30, bf16[32,32,128]{2,1,0:T(8,128)(2,1)S(1)} %get-tuple-element.94), kind=kOutput, calls=%fused_computation.4.clone.1 | convolution fusion | flops 3222798336 | bytes 28574208 | tf_op jit(solution)/shard_map/while/body/eval_jaxpr/icjd,cde->ije/dot_general | solution.py:37
  760.0 258.0 %reduce-scatter.2.cloned.1.call-done = bf16[96,384,128]{2,1,0:T(8,128)(2,1)} async-done(((bf16[384,384,128]{2,1,0:T(8,128)(2,1)}), bf16[96,384,128]{2,1,0:T(8,128)(2,1)}) %reduce-scatter.2.cloned.1.call-update) | async-done | bytes 9437200 | tf_op jit(solution)/shard_map/reduce_scatter | solution.py:61
  1018.6 324.4 %all-reduce.2.cloned.1.call-done = bf16[96,384,128]{2,1,0:T(8,128)(2,1)} async-done(((bf16[96,384,128]{2,1,0:T(8,128)(2,1)}), bf16[96,384,128]{2,1,0:T(8,128)(2,1)}) %all-reduce.2.cloned.1.call-update) | async-done | bytes 9437200 | tf_op jit(solution)/shard_map/psum | solution.py:62
  1343.0 20.2 %divide_add_fusion = f32[96,384,128]{2,1,0:T(8,128)} fusion(f32[96,384,128]{2,1,0:T(8,128)} %param.15, bf16[96,384,128]{2,1,0:T(8,128)(2,1)} %all-reduce.2.cloned.1.call-done, f32[96,384]{1,0:T(8,128)S(1)} %convolution_add_fusion.2, f32[128]{0:T(128)S(1)} %convert_element_type.64), kind=kLoop, calls=%fused_computation.17 | loop fusion | flops 18874368 | bytes 47333888 | tf_op jit(solution)/shard_map/add | solution.py:67
  (76 shorter events, 165.7 us)
Async XLA Ops:
  7.2 193.6 %copy-start = (bf16[256,32]{0,1:T(8,128)(2,1)S(1)}, bf16[256,32]{0,1:T(8,128)(2,1)}, u32[]{:S(2)}) copy-start(bf16[256,32]{0,1:T(8,128)(2,1)} %param.18) | copy-start | bytes 49156
  7.2 8.0 copy-start.6
  7.2 8.0 copy-start.7
  7.2 8.0 copy-start.8
  7.2 8.1 copy-start.9
  7.2 144.9 %all-to-all-start = ((bf16[256,96,256]{2,1,0:T(8,128)(2,1)}), bf16[256,96,256]{2,1,0:T(8,128)(2,1)}, u32[]{:S(2)}, u32[]{:S(2)}) async-start(bf16[256,96,256]{2,1,0:T(8,128)(2,1)} %param.13), calls=%async_computation | async-start | bytes 25165824 | tf_op jit(solution)/shard_map/all_to_all | solution.py:51
  13.7 1004.3 %reduce-scatter.2.cloned.1.call-start = ((), (), s32[]{:S(2)}) async-start(), calls=%async_computation.2 | async-start | bytes 47185920 | tf_op jit(solution)/shard_map/reduce_scatter | solution.py:61
  196.3 4.5 copy-start.2
  225.4 12.8 copy-start.4
  253.1 10.3 copy-start.5
  759.9 258.1 %copy-start.3 = (s32[1024,384]{1,0:T(8,128)S(1)}, s32[1024,384]{1,0:T(8,128)}, u32[]{:S(2)}) copy-start(s32[1024,384]{1,0:T(8,128)} %param.14) | copy-start | bytes 4718596
  759.9 258.2 %copy-start.10 = (bf16[128]{0:T(256)(128)(2,1)S(1)}, bf16[128]{0:T(256)(128)(2,1)}, u32[]{:S(2)}) copy-start(bf16[128]{0:T(256)(128)(2,1)} %param.23) | copy-start | bytes 772
  759.9 583.1 %all-reduce.2.cloned.1.call-start = ((), (), s32[]{:S(2)}) async-start(), calls=%async_computation.3 | async-start | bytes 18874368 | tf_op jit(solution)/shard_map/psum | solution.py:62
  1018.1 345.1 %copy-start.1 = (bf16[256,32]{0,1:T(8,128)(2,1)S(1)}, bf16[256,32]{0,1:T(8,128)(2,1)}, u32[]{:S(2)}) copy-start(bf16[256,32]{0,1:T(8,128)(2,1)} %param.18) | copy-start | bytes 49156
Sparse Core Ops, SparseCore 0:
  760.0 257.8 reduce-scatter.1
  1020.4 322.5 all-reduce.1
where the time goes:
time: 1370 us
  waiting for transfers between devices  719 us (52%)
  matrix products  426 us (31%)
  local copies, waits for them, and re-layouts  119 us (9%)
  other arithmetic  84 us (6%)
  between operations  14.3 us (1%)
    psum x1, waiting for transfers between devices, local_fn(): summed = lax.psum(summed, 'seq')  324 us
    dot_general x12, matrix products, one_block(): jnp.einsum('icjd,cde->ije', outer_blk, w_out3, preferred_element_type=jnp...  271 us
    reduce_scatter x1, waiting for transfers between devices, local_fn(): summed = lax.psum_scatter(partial, 'dap', scatter_dimension=0, tiled=True)  258 us
    dot_general x12, matrix products, one_block(): jnp.einsum('sic,sjd->icjd', left_blk, right_proj, preferred_element_type=...  141 us
    all_to_all x1, waiting for transfers between devices, local_fn(): local_c7 = lax.all_to_all(array_b7, 'dap', 0, 1, tiled=True)  137 us
    another operation x12, local copies, waits for them, and re-layouts  71.1 us
  transfers between devices with their start and end apart: 3, of which 3 were waited for; matrix products, arithmetic and copies ran while one was open for 0% of the time, Pallas kernels for 0%

commit v1 on v0

v1 whole, which is shorter than its diff:
```python
import functools
import jax
import jax.numpy as jnp
from jax import lax
from jax.experimental import pallas as pl
from jax.experimental.pallas import tpu as pltpu
from jax.sharding import PartitionSpec as P

MESH = pl.DeviceIdType.MESH
BF16 = jnp.bfloat16
F32 = jnp.float32

NZ = 4
LOC_S = 256
LOC_R = 96
PAD_R = 128
N_RES = 384
C_M = 256
C_H = 32
C_Z = 128
RB = 8
N_RB = LOC_R // RB
N_Q = 4
N_TILES = N_RB * N_Q
LAG = 2
N_STEPS = N_TILES + 3 * LAG
P_SLOTS = 8
S_SLOTS = 4
D_CHUNK = 8
PRO_R = 16
PRO_S = 32


def project_kernel(m_ref, mask_ref, gamma_ref, beta_ref, w_ref, bias_ref, at_ref, bt_ref, xs_ref, bs_ref):
    gamma = gamma_ref[...].reshape(1, 1, C_M)
    beta = beta_ref[...].reshape(1, 1, C_M)

    def norm(step, carry):
        start = pl.multiple_of(step * PRO_S, PRO_S)
        x = m_ref[pl.ds(start, PRO_S)].astype(F32)
        mean = jnp.mean(x, axis=-1, keepdims=True)
        cent = x - mean
        var = jnp.mean(cent * cent, axis=-1, keepdims=True)
        y = cent * lax.rsqrt(var + 1e-5) * gamma + beta
        xs_ref[:, pl.ds(start, PRO_S), :] = jnp.swapaxes(y, 0, 1).astype(BF16)
        return carry

    lax.fori_loop(0, LOC_S // PRO_S, norm, 0)
    for r in range(PRO_R):
        t = lax.dot_general(w_ref[...], xs_ref[r], (((1,), (1,)), ((), ())), preferred_element_type=F32)
        t = (t + bias_ref[...]) * mask_ref[r:r + 1, :]
        at_ref[r * C_H:(r + 1) * C_H, :] = t[:C_H].astype(BF16)
        bs_ref[r] = t[C_H:]
    bt_ref[...] = jnp.swapaxes(bs_ref[...], 0, 1).astype(BF16)


def project(m, mask_t, gamma, beta, w_t, bias):
    return pl.pallas_call(
        project_kernel,
        grid=(LOC_R // PRO_R,),
        in_specs=[
            pl.BlockSpec((LOC_S, PRO_R, C_M), lambda i: (0, i, 0)),
            pl.BlockSpec((PRO_R, LOC_S), lambda i: (i, 0)),
            pl.BlockSpec((1, C_M), lambda i: (0, 0)),
            pl.BlockSpec((1, C_M), lambda i: (0, 0)),
            pl.BlockSpec((2 * C_H, C_M), lambda i: (0, 0)),
            pl.BlockSpec((2 * C_H, 1), lambda i: (0, 0)),
        ],
        out_specs=[
            pl.BlockSpec((PRO_R * C_H, LOC_S), lambda i: (i, 0)),
            pl.BlockSpec((C_H, PRO_R, LOC_S), lambda i: (0, i, 0)),
        ],
        out_shape=[
            jax.ShapeDtypeStruct((LOC_R * C_H, LOC_S), BF16),
            jax.ShapeDtypeStruct((C_H, LOC_R, LOC_S), BF16),
        ],
        scratch_shapes=[
            pltpu.VMEM((PRO_R, LOC_S, C_M), BF16),
            pltpu.VMEM((PRO_R, C_H, LOC_S), F32),
        ],
        compiler_params=pltpu.CompilerParams(vmem_limit_bytes=40 * 2**20),
        name="project",
    )(m, mask_t, gamma, beta, w_t, bias)


def main_kernel(m_hbm, at_ref, bt_hbm, wt_ref, inv_ref, bo_ref, z_hbm,
                zo_hbm, mo_hbm,
                b_all, o_buf, p_buf, from_left, from_right, to_right, to_left, z_in, z_out,
                b_send, b_recv, b_local, m_send, m_recv, m_local,
                r_send, r_recv, l_send, l_recv, zi_sem, zo_sem):
    data = lax.axis_index('data')
    z = lax.axis_index('seq')
    d = lax.axis_index('dap')
    core = lax.rem(d, 2)
    chip = lax.div(d, 2)
    sib = chip * 2 + (1 - core)
    far = (1 - chip) * 2 + core
    far_sib = (1 - chip) * 2 + (1 - core)

    def dev(seq, dap):
        return (data, seq, dap)

    barrier = pltpu.get_barrier_semaphore()
    for peer in (sib, far, far_sib):
        pl.semaphore_signal(barrier, inc=1, device_id=dev(z, peer), device_id_type=MESH)

    @pl.when(z > 0)
    def _():
        pl.semaphore_signal(barrier, inc=1, device_id=dev(z - 1, d), device_id_type=MESH)

    @pl.when(z < NZ - 1)
    def _():
        pl.semaphore_signal(barrier, inc=1, device_id=dev(z + 1, d), device_id_type=MESH)

    at_end = jnp.logical_or(z == 0, z == NZ - 1)
    pl.semaphore_wait(barrier, jnp.where(at_end, 4, 5))

    b_own = pltpu.make_async_copy(bt_hbm, b_all.at[0, :, pl.ds(0, LOC_R), :], b_local)
    b_own.start()

    def b_copy(src, q, peer):
        return pltpu.make_async_remote_copy(
            src_ref=src, dst_ref=b_all.at[q, :, pl.ds(0, LOC_R), :],
            send_sem=b_send.at[q], recv_sem=b_recv.at[q],
            device_id=dev(z, peer), device_id_type=MESH)

    b_sib = b_copy(bt_hbm, 1, sib)
    b_far = b_copy(bt_hbm, 2, far)
    b_relay = b_copy(b_all.at[2, :, pl.ds(0, LOC_R), :], 3, sib)
    b_far.start()
    b_sib.start()

    def m_copy(k, peer):
        rows = m_hbm.shape[0] // 4
        return pltpu.make_async_remote_copy(
            src_ref=m_hbm.at[pl.ds(peer * rows, rows)],
            dst_ref=mo_hbm.at[:, pl.ds(pl.multiple_of(d * LOC_R, LOC_R), LOC_R), :],
            send_sem=m_send.at[k], recv_sem=m_recv.at[k],
            device_id=dev(z, peer), device_id_type=MESH)

    rows = m_hbm.shape[0] // 4
    m_copies = [m_copy(0, sib), m_copy(1, far), m_copy(2, far_sib)]
    for cp in m_copies:
        cp.start()
    m_own = pltpu.make_async_copy(
        m_hbm.at[pl.ds(d * rows, rows)],
        mo_hbm.at[:, pl.ds(pl.multiple_of(d * LOC_R, LOC_R), LOC_R), :], m_local)
    m_own.start()

    b_all[:, :, LOC_R:, :] = jnp.zeros((N_Q, C_H, PAD_R - LOC_R, LOC_S), BF16)
    b_own.wait()

    def columns(q):
        c2 = lax.rem(core + lax.rem(q, 2), 2)
        y2 = lax.rem(chip + lax.div(q, 2), 2)
        return pl.multiple_of((2 * y2 + c2) * LOC_R, LOC_R)

    def tile_of(t):
        return lax.div(t, N_RB), lax.rem(t, N_RB)

    def compute(t):
        q, rb = tile_of(t)
        slot = lax.rem(t, P_SLOTS)
        a_blk = at_ref[pl.ds(pl.multiple_of(rb * RB * C_H, RB * C_H), RB * C_H), :]
        acc = [None] * (RB // 2)
        for ch in range(C_H // D_CHUNK):
            b_blk = b_all[q, ch * D_CHUNK:(ch + 1) * D_CHUNK].reshape(D_CHUNK * PAD_R, LOC_S)
            o = lax.dot_general(a_blk, b_blk, (((1,), (1,)), ((), ())), preferred_element_type=F32).astype(BF16)
            for i in range(RB):
                for dd in range(D_CHUNK):
                    o_buf[i // 2, dd * C_H:(dd + 1) * C_H, (i % 2) * PAD_R:(i % 2 + 1) * PAD_R] = (
                        o[i * C_H:(i + 1) * C_H, dd * PAD_R:(dd + 1) * PAD_R])
            w_blk = wt_ref[:, ch * D_CHUNK * C_H:(ch + 1) * D_CHUNK * C_H]
            for p in range(RB // 2):
                r = jnp.dot(w_blk, o_buf[p], preferred_element_type=F32)
                acc[p] = r if acc[p] is None else acc[p] + r
        for p in range(RB // 2):
            for i in range(2):
                p_buf[slot, 2 * p + i] = acc[p][:, i * PAD_R:(i + 1) * PAD_R].T[:LOC_R]

    def right_copy(t):
        slot = lax.rem(t, S_SLOTS)
        return pltpu.make_async_remote_copy(
            src_ref=to_right.at[slot], dst_ref=from_left.at[t],
            send_sem=r_send.at[slot], recv_sem=r_recv.at[t],
            device_id=dev(z + 1, d), device_id_type=MESH)

    def left_copy(t):
        slot = lax.rem(t, S_SLOTS)
        return pltpu.make_async_remote_copy(
            src_ref=to_left.at[slot], dst_ref=from_right.at[t],
            send_sem=l_send.at[slot], recv_sem=l_recv.at[t],
            device_id=dev(z - 1, d), device_id_type=MESH)

    def z_window(ref, t):
        q, rb = tile_of(t)
        return ref.at[pl.ds(pl.multiple_of(rb * RB, RB), RB), pl.ds(columns(q), LOC_R), :]

    def z_fetch(t):
        slot = lax.rem(t, 2)
        return pltpu.make_async_copy(z_window(z_hbm, t), z_in.at[slot], zi_sem.at[slot])

    def z_write(t):
        slot = lax.rem(t, 2)
        return pltpu.make_async_copy(z_out.at[slot], z_window(zo_hbm, t), zo_sem.at[slot])

    lag_right = z * LAG
    lag_left = (NZ - 1 - z) * LAG
    lag_end = jnp.maximum(lag_right, lag_left)

    def step(n, carry):
        @pl.when(n == N_RB)
        def _():
            b_sib.wait_recv()

        @pl.when(n == N_RB + 2)
        def _():
            b_far.wait_recv()
            b_relay.start()

        @pl.when(n == 3 * N_RB)
        def _():
            b_relay.wait_recv()

        @pl.when(n < N_TILES)
        def _():
            compute(n)

        tr = n - lag_right
        right_on = jnp.logical_and(tr >= 0, tr < N_TILES)
        tl = n - lag_left
        left_on = jnp.logical_and(tl >= 0, tl < N_TILES)
        send_right = jnp.logical_and(right_on, z < NZ - 1)
        send_left = jnp.logical_and(left_on, z > 0)

        @pl.when(jnp.logical_and(right_on, z > 0))
        def _():
            pltpu.make_async_remote_copy(
                src_ref=to_right.at[0], dst_ref=from_left.at[tr],
                send_sem=r_send.at[0], recv_sem=r_recv.at[tr],
                device_id=dev(z - 1, d), device_id_type=MESH).wait_recv()

        @pl.when(jnp.logical_and(left_on, z < NZ - 1))
        def _():
            pltpu.make_async_remote_copy(
                src_ref=to_left.at[0], dst_ref=from_right.at[tl],
                send_sem=l_send.at[0], recv_sem=l_recv.at[tl],
                device_id=dev(z + 1, d), device_id_type=MESH).wait_recv()

        @pl.when(jnp.logical_and(send_right, tr >= S_SLOTS))
        def _():
            right_copy(tr - S_SLOTS).wait_send()

        @pl.when(jnp.logical_and(send_left, tl >= S_SLOTS))
        def _():
            left_copy(tl - S_SLOTS).wait_send()

        @pl.when(jnp.logical_and(send_right, z == 0))
        def _():
            to_right[lax.rem(tr, S_SLOTS)] = p_buf[lax.rem(tr, P_SLOTS)].astype(BF16)

        @pl.when(jnp.logical_and(send_right, z > 0))
        def _():
            to_right[lax.rem(tr, S_SLOTS)] = (
                p_buf[lax.rem(tr, P_SLOTS)] + from_left[tr].astype(F32)).astype(BF16)

        @pl.when(jnp.logical_and(send_left, z == NZ - 1))
        def _():
            to_left[lax.rem(tl, S_SLOTS)] = p_buf[lax.rem(tl, P_SLOTS)].astype(BF16)

        @pl.when(jnp.logical_and(send_left, z < NZ - 1))
        def _():
            to_left[lax.rem(tl, S_SLOTS)] = (
                p_buf[lax.rem(tl, P_SLOTS)] + from_right[tl].astype(F32)).astype(BF16)

        @pl.when(send_right)
        def _():
            right_copy(tr).start()

        @pl.when(send_left)
        def _():
            left_copy(tl).start()

        te = n - lag_end

        @pl.when(jnp.logical_and(te >= -1, te < N_TILES - 1))
        def _():
            z_fetch(te + 1).start()

        @pl.when(jnp.logical_and(te >= 0, te < N_TILES))
        def _():
            q, rb = tile_of(te)
            slot = lax.rem(te, 2)
            z_fetch(te).wait()

            @pl.when(te >= 2)
            def _():
                z_write(te - 2).wait()

            def finish(i, total):
                inv = inv_ref[rb, pl.ds(columns(q), LOC_R), :]
                z_out[slot, i] = z_in[slot, i] + (total + bo_ref[...]) * inv[:, i:i + 1]

            p_slot = lax.rem(te, P_SLOTS)

            @pl.when(z == 0)
            def _():
                for i in range(RB):
                    finish(i, p_buf[p_slot, i] + from_right[te, i].astype(F32))

            @pl.when(z == NZ - 1)
            def _():
                for i in range(RB):
                    finish(i, p_buf[p_slot, i] + from_left[te, i].astype(F32))

            @pl.when(jnp.logical_and(z > 0, z < NZ - 1))
            def _():
                for i in range(RB):
                    finish(i, p_buf[p_slot, i] + from_left[te, i].astype(F32) + from_right[te, i].astype(F32))

            z_write(te).start()

        return carry

    lax.fori_loop(0, N_STEPS, step, 0)

    @pl.when(z < NZ - 1)
    def _():
        for k in range(S_SLOTS):
            right_copy(N_TILES - S_SLOTS + k).wait_send()

    @pl.when(z > 0)
    def _():
        for k in range(S_SLOTS):
            left_copy(N_TILES - S_SLOTS + k).wait_send()

    z_write(N_TILES - 2).wait()
    z_write(N_TILES - 1).wait()
    b_sib.wait_send()
    b_far.wait_send()
    b_relay.wait_send()
    m_own.wait()
    for cp in m_copies:
        cp.wait()


def combine(m, a_t, b_t, w_t, inv, b_out, pair):
    any_spec = pl.BlockSpec(memory_space=pl.ANY)
    vmem_spec = pl.BlockSpec(memory_space=pltpu.VMEM)
    dma = pltpu.SemaphoreType.DMA
    return pl.pallas_call(
        main_kernel,
        in_specs=[any_spec, vmem_spec, any_spec, vmem_spec, vmem_spec, vmem_spec, any_spec],
        out_specs=[any_spec, any_spec],
        out_shape=[
            jax.ShapeDtypeStruct((LOC_R, N_RES, C_Z), F32),
            jax.ShapeDtypeStruct((LOC_S // 4, N_RES, C_M), BF16),
        ],
        scratch_shapes=[
            pltpu.VMEM((N_Q, C_H, PAD_R, LOC_S), BF16),
            pltpu.VMEM((RB // 2, D_CHUNK * C_H, 2 * PAD_R), BF16),
            pltpu.VMEM((P_SLOTS, RB, LOC_R, C_Z), F32),
            pltpu.VMEM((N_TILES, RB, LOC_R, C_Z), BF16),
            pltpu.VMEM((N_TILES, RB, LOC_R, C_Z), BF16),
            pltpu.VMEM((S_SLOTS, RB, LOC_R, C_Z), BF16),
            pltpu.VMEM((S_SLOTS, RB, LOC_R, C_Z), BF16),
            pltpu.VMEM((2, RB, LOC_R, C_Z), F32),
            pltpu.VMEM((2, RB, LOC_R, C_Z), F32),
            dma((4,)), dma((4,)), dma, dma((3,)), dma((3,)), dma,
            dma((S_SLOTS,)), dma((N_TILES,)), dma((S_SLOTS,)), dma((N_TILES,)), dma((2,)), dma((2,)),
        ],
        compiler_params=pltpu.CompilerParams(
            collective_id=0, has_side_effects=True, vmem_limit_bytes=60 * 2**20),
        name="combine",
    )(m, a_t, b_t, w_t, inv, b_out, pair)


def solution(mesh):
    rep = P()
    in_specs = (P(('data', 'seq'), 'dap', None), P('data', None), P(('data', 'dap'), None, None)) + (rep,) * 8
    out_specs = (P(('data', 'dap'), None, None), P(('data', 'seq', 'dap'), None, None))

    def local_fn(m, mask, pair, ln_gamma, ln_beta, w_left, b_left, w_right, b_right, w_out, b_out):
        seq_idx = lax.axis_index('seq')
        dap_idx = lax.axis_index('dap')
        mask_cols = lax.dynamic_slice_in_dim(mask, dap_idx * LOC_R, LOC_R, axis=1)
        mask_t = lax.dynamic_slice_in_dim(mask_cols, seq_idx * LOC_S, LOC_S, axis=0).astype(F32).T
        w_t = jnp.concatenate([w_left, w_right], axis=1).T
        bias = jnp.concatenate([b_left, b_right]).astype(F32)[:, None]
        a_t, b_t = project(m, mask_t, ln_gamma.astype(F32)[None], ln_beta.astype(F32)[None], w_t, bias)
        count = jnp.einsum('si,sj->ij', mask_cols.astype(BF16), mask.astype(BF16), preferred_element_type=F32)
        inv = (1.0 / (1e-3 + count)).reshape(N_RB, RB, N_RES).transpose(0, 2, 1)
        wo_t = w_out.reshape(C_H, C_H, C_Z).transpose(2, 1, 0).reshape(C_Z, C_H * C_H)
        pair_out, msa_out = combine(m, a_t, b_t, wo_t, inv, b_out.astype(F32)[None], pair)
        return pair_out, msa_out

    return jax.shard_map(local_fn, mesh=mesh, in_specs=in_specs, out_specs=out_specs, check_vma=False)
```

time: 1370 us -> 287 us (0.21)
  waiting for transfers between devices: 719 us -> 0 us
  matrix products: 426 us -> 2.36 us
  Pallas kernels: 0 us -> 252 us
  local copies, waits for them, and re-layouts: 119 us -> 27.9 us
  other arithmetic: 84 us -> 4.05 us
    dot_general x27 -> x1, matrix products: 426 us -> 2.36 us  [local_fn(): jnp.einsum('si,sj->ij', mask_cols.astype(BF16), mask.astype(BF16), prefer...]
    psum x1 -> x0, waiting for transfers between devices: 324 us -> none  [local_fn(): summed = lax.psum(summed, 'seq')]
    reduce_scatter x1 -> x0, waiting for transfers between devices: 258 us -> none  [local_fn(): summed = lax.psum_scatter(partial, 'dap', scatter_dimension=0, tiled=True)]
    pallas_call x0 -> x2, Pallas kernels: none -> 252 us  [the longest x1 229 us: combine(): pl.pallas_call(main_kernel, in_specs=[any_spec, vmem_spec, any_spec, vmem...]
    all_to_all x1 -> x0, waiting for transfers between devices: 137 us -> none  [local_fn(): local_c7 = lax.all_to_all(array_b7, 'dap', 0, 1, tiled=True)]
    another operation x12 -> x0, local copies, waits for them, and re-layouts: 71.1 us -> none
    convert_element_type x9 -> x1, other arithmetic: 23.8 us -> 0.79 us  [local_fn(): bias = jnp.concatenate([b_left, b_right]).astype(F32)[:, None]]
    add x1 -> x0, other arithmetic: 20.2 us -> none  [local_fn(): return (pair_rows + update, local_c7)]
  transfers between devices with their start and end apart: 3 -> 0, of which waited for: 3 -> 0; matrix products, arithmetic and copies ran while one was open for 0% -> 0% of each run, Pallas kernels for 0% -> 0%
where the time goes in v1:
time: 287 us
  Pallas kernels  252 us (88%)
  local copies, waits for them, and re-layouts  27.9 us (10%)
  other arithmetic  4.05 us (1%)
    pallas_call x1, Pallas kernels, combine(): pl.pallas_call(main_kernel, in_specs=[any_spec, vmem_spec, any_spec, vmem...  229 us
    unnamed x11, local copies, waits for them, and re-layouts  23.7 us
    pallas_call x1, Pallas kernels, project(): pl.pallas_call(project_kernel, grid=(LOC_R // PRO_R,), in_specs=[pl.Block...  22.8 us

profile of v1, /device:TPU:0, one launch (start us, length us, event | category | flops | bytes accessed | tf_op | source)
XLA Modules:
  0.0 286.7 jit_solution(3050651113534368830)
XLA Ops:
  0.6 0.0 copy-start.3
  0.7 0.8 maximum_convert_fusion
  1.4 1.2 bitcast_convert_fusion.bo_ref
  2.6 0.7 broadcast_in_dim.22
  3.3 0.7 broadcast_in_dim.23
  4.0 0.1 copy.34.bias_ref
  4.0 0.7 maximum_bitcast_fusion.w_ref
  4.8 1.1 dynamic_slice.6
  5.8 0.1 copy.38
  6.0 2.4 fusion.1
  8.3 0.0 copy-done.3
  8.3 0.1 copy.35
  8.4 0.8 copy.37.wt_ref
  9.3 2.1 copy.36
  11.4 22.8 %project.1 = (bf16[3072,256]{1,0:T(8,128)(2,1)S(1)}, bf16[32,96,256]{2,1,0:T(8,128)(2,1)S(1)}) custom-call(bf16[256,96,256]{2,1,0:T(8,128)(2,1)} %m_hbm.1, f32[96,256]{1,0:T(8,128)S(1)} %convert_bitcast_fusion.mask_ref, f32[1,256]{1,0:T(1,128)S(1)} %bitcast.18, f32[1,256]{1,0:T(1,128)S(1)} %bitcast.19, bf16[64,256]{1,0:T(8,128)(2,1)S(1)} %maximum_bitcast_fusion.w_ref, ...), custom_call_target="tpu_custom_call" | custom-call | tf_op jit(solution)/shard_map/project/pallas_call | solution.py:58
  34.2 0.0 copy-start
  34.2 1.1 copy-done
  35.3 0.0 copy-start.1
  35.3 1.2 copy-done.1
  36.5 228.8 %combine.1 = (f32[96,384,128]{2,1,0:T(8,128)}, bf16[64,384,256]{2,1,0:T(8,128)(2,1)}) custom-call(bf16[256,96,256]{2,1,0:T(8,128)(2,1)} %m_hbm.1, bf16[3072,256]{1,0:T(8,128)(2,1)} %copy-done, bf16[32,96,256]{2,1,0:T(8,128)(2,1)} %copy-done.1, bf16[128,1024]{1,0:T(8,128)(2,1)} %copy.37.wt_ref, f32[12,384,8]{2,1,0:T(8,128)} %bitcast.20, ...), custom_call_target="tpu_custom_call" | custom-call | tf_op jit(solution)/shard_map/combine/pallas_call | solution.py:351
  265.3 0.0 copy-start.2
  265.4 13.8 %copy.41 = f32[96,384,128]{2,1,0:T(8,128)} copy(f32[96,384,128]{2,1,0:T(8,128)} %get-tuple-element.8) | data formatting | bytes 37748736
  279.2 2.7 copy-done.2
  281.9 4.8 %copy.42 = bf16[64,384,256]{2,1,0:T(8,128)(2,1)} copy(bf16[64,384,256]{2,1,0:T(8,128)(2,1)S(1)} %copy-done.2) | data formatting | bytes 25165824
  (1 shorter events, 0.0 us)
Async XLA Ops:
  0.6 7.7 %copy-start.3 = (bf16[1024,128]{1,0:T(8,128)(2,1)S(1)}, bf16[1024,128]{1,0:T(8,128)(2,1)}, u32[]{:S(2)}) copy-start(bf16[1024,128]{1,0:T(8,128)(2,1)} %param.20) | copy-start | bytes 786436
  34.2 1.1 copy-start
  35.3 1.2 copy-start.1
  265.3 16.6 %copy-start.2 = (bf16[64,384,256]{2,1,0:T(8,128)(2,1)S(1)}, bf16[64,384,256]{2,1,0:T(8,128)(2,1)}, u32[]{:S(2)}) copy-start(bf16[64,384,256]{2,1,0:T(8,128)(2,1)} %get-tuple-element.9) | copy-start | bytes 37748740

commit v2 on v0

v2 whole, which is shorter than its diff:
```python
import jax
import jax.numpy as jnp
from jax import lax
from jax.experimental import pallas as pl
from jax.experimental.pallas import tpu as pltpu
from jax.sharding import PartitionSpec as P

MESH = pl.DeviceIdType.MESH
BF16 = jnp.bfloat16
F32 = jnp.float32

NZ = 4
N_SEQ = 1024
LOC_S = 256
LOC_R = 96
PAD_R = 128
N_RES = 384
C_M = 256
C_H = 32
C_Z = 128
RB = 8
N_RB = LOC_R // RB
N_Q = 4
N_BLOCKS = N_RB * N_Q
UR = 4
UPB = RB // UR
N_UNITS = N_BLOCKS * UPB
LAG = 3
N_STEPS = N_UNITS + 3 * LAG
P_SLOTS = 16
R_SLOTS = 16
S_SLOTS = 6
D_CHUNK = 8
PRO_R = 16
HALF_S = 128
PRO_S = 16
PITCH = 2 * LOC_S + 1


def main_kernel(m_hbm, mask_hbm, gamma_ref, beta_ref, bl_ref, br_ref, bo_ref, wl_ref, wr_ref, wo_ref, z_hbm,
                zo_ref, mo_ref,
                b_all, at_ref, o_buf, p_buf, inv_buf, from_left, from_right, to_right, to_left, z_in,
                mask_ref, mask_t, m_buf, xs_ref, bs_ref, wp_ref, wt_ref, bias_ref,
                b_send, b_recv, m_send, m_recv, m_local,
                r_send, r_recv, l_send, l_recv, zi_sem, mb_sem, mask_sem):
    data = lax.axis_index('data')
    z = lax.axis_index('seq')
    d = lax.axis_index('dap')
    core = lax.rem(d, 2)
    chip = lax.div(d, 2)
    sib = chip * 2 + (1 - core)
    far = (1 - chip) * 2 + core
    far_sib = (1 - chip) * 2 + (1 - core)

    def dev(seq, dap):
        return (data, seq, dap)

    barrier = pltpu.get_barrier_semaphore()
    for peer in (sib, far, far_sib):
        pl.semaphore_signal(barrier, inc=1, device_id=dev(z, peer), device_id_type=MESH)

    @pl.when(z > 0)
    def _():
        pl.semaphore_signal(barrier, inc=1, device_id=dev(z - 1, d), device_id_type=MESH)

    @pl.when(z < NZ - 1)
    def _():
        pl.semaphore_signal(barrier, inc=1, device_id=dev(z + 1, d), device_id_type=MESH)

    def m_fetch(k, half):
        return pltpu.make_async_copy(
            m_hbm.at[pl.ds(half * HALF_S, HALF_S), pl.ds(pl.multiple_of(k * PRO_R, PRO_R), PRO_R), :],
            m_buf.at[half], mb_sem.at[half])

    def mask_fetch(k):
        return pltpu.make_async_copy(
            mask_hbm.at[pl.ds(pl.multiple_of(k * 128, 128), 128)], mask_ref.at[lax.rem(k, 2)], mask_sem.at[lax.rem(k, 2)])

    mask_fetch(0).start()
    mask_fetch(1).start()
    m_fetch(0, 0).start()
    m_fetch(0, 1).start()

    def eye(n):
        return (lax.broadcasted_iota(jnp.int32, (n, n), 0) == lax.broadcasted_iota(jnp.int32, (n, n), 1))

    def column(ref):
        return jnp.sum(jnp.where(eye(C_H), ref[...].astype(F32).reshape(1, C_H), 0.0), axis=1, keepdims=True)

    wp_ref[:C_H] = wl_ref[...]
    wp_ref[C_H:] = wr_ref[...]
    bias_ref[:C_H] = column(bl_ref)
    bias_ref[C_H:] = column(br_ref)
    wo = jnp.swapaxes(wo_ref[...].astype(F32).reshape(C_H, C_H, C_Z), 0, 1).reshape(C_H * C_H, C_Z)
    wt_ref[...] = lax.dot_general(eye(C_Z).astype(F32).astype(BF16), wo.astype(BF16), (((1,), (1,)), ((), ())),
                                  preferred_element_type=F32).astype(BF16)
    gamma = gamma_ref[...].astype(F32).reshape(1, 1, C_M)
    beta = beta_ref[...].astype(F32).reshape(1, 1, C_M)
    bo = bo_ref[...].astype(F32).reshape(1, C_Z)

    b_all[:, :, LOC_R:, :] = jnp.zeros((N_Q, C_H, PAD_R - LOC_R, LOC_S), BF16)

    def flip(k, carry):
        mask_fetch(k).wait()
        mask_t[:, pl.ds(pl.multiple_of(k * 128, 128), 128)] = mask_ref[lax.rem(k, 2)].astype(F32).T

        @pl.when(k < N_SEQ // 128 - 2)
        def _():
            mask_fetch(k + 2).start()

        return carry

    lax.fori_loop(0, N_SEQ // 128, flip, 0)

    at_end = jnp.logical_or(z == 0, z == NZ - 1)
    pl.semaphore_wait(barrier, jnp.where(at_end, 4, 5))

    rows = m_hbm.shape[0] // 4
    m_place = mo_ref.at[:, pl.ds(pl.multiple_of(d * LOC_R, LOC_R), LOC_R), :]

    def m_copy(k, peer):
        return pltpu.make_async_remote_copy(
            src_ref=m_hbm.at[pl.ds(peer * rows, rows)], dst_ref=m_place,
            send_sem=m_send.at[k], recv_sem=m_recv.at[k],
            device_id=dev(z, peer), device_id_type=MESH)

    m_copies = [m_copy(0, sib), m_copy(1, far), m_copy(2, far_sib)]
    m_own = pltpu.make_async_copy(m_hbm.at[pl.ds(d * rows, rows)], m_place, m_local)

    def project(k, carry):
        for half in range(2):
            m_fetch(k, half).wait()

            def norm(step, c2):
                start = pl.multiple_of(step * PRO_S, PRO_S)
                x = m_buf[half, pl.ds(start, PRO_S)].astype(F32)
                mean = jnp.mean(x, axis=-1, keepdims=True)
                cent = x - mean
                var = jnp.mean(cent * cent, axis=-1, keepdims=True)
                y = cent * lax.rsqrt(var + 1e-5) * gamma + beta
                for s in range(PRO_S):
                    for lanes in range(2):
                        xs_ref[pl.ds(2 * (half * HALF_S + start + s) + lanes, PRO_R, stride=PITCH), :] = (
                            y[s, :, lanes * 128:(lanes + 1) * 128])
                return c2

            lax.fori_loop(0, HALF_S // PRO_S, norm, 0)

            @pl.when(k < LOC_R // PRO_R - 1)
            def _():
                m_fetch(k + 1, half).start()

        mask_rows = mask_t[pl.ds(pl.multiple_of(d * LOC_R + k * PRO_R, PRO_R), PRO_R),
                           pl.ds(pl.multiple_of(z * LOC_S, LOC_S), LOC_S)]
        for r in range(PRO_R):
            x = jnp.concatenate([xs_ref[pl.ds(r * PITCH + lanes, LOC_S, stride=2), :] for lanes in range(2)], axis=1)
            t = lax.dot_general(wp_ref[...], x.astype(BF16), (((1,), (1,)), ((), ())), preferred_element_type=F32)
            t = (t + bias_ref[...]) * mask_rows[r:r + 1]
            at_ref[pl.ds(pl.multiple_of((k * PRO_R + r) * C_H, C_H), C_H), :] = t[:C_H].astype(BF16)
            bs_ref[r] = t[C_H:]
        b_all[0, :, pl.ds(pl.multiple_of(k * PRO_R, PRO_R), PRO_R), :] = (
            jnp.swapaxes(bs_ref[...], 0, 1).astype(BF16))
        return carry

    lax.fori_loop(0, LOC_R // PRO_R, project, 0)

    def b_copy(src_q, q, peer):
        return pltpu.make_async_remote_copy(
            src_ref=b_all.at[src_q, :, pl.ds(0, LOC_R), :], dst_ref=b_all.at[q, :, pl.ds(0, LOC_R), :],
            send_sem=b_send.at[q], recv_sem=b_recv.at[q],
            device_id=dev(z, peer), device_id_type=MESH)

    b_sib = b_copy(0, 1, sib)
    b_far = b_copy(0, 2, far)
    b_relay = b_copy(2, 3, sib)

    def columns(q):
        c2 = lax.rem(core + lax.rem(q, 2), 2)
        y2 = lax.rem(chip + lax.div(q, 2), 2)
        return pl.multiple_of((2 * y2 + c2) * LOC_R, LOC_R)

    def block_of(b):
        return lax.div(b, N_RB), lax.rem(b, N_RB)

    def compute(b):
        q, rb = block_of(b)
        slot = lax.rem(b, P_SLOTS // UPB) * UPB
        a_blk = at_ref[pl.ds(pl.multiple_of(rb * RB * C_H, RB * C_H), RB * C_H), :]
        acc = [None] * (RB // 2)
        for ch in range(C_H // D_CHUNK):
            b_blk = b_all[q, ch * D_CHUNK:(ch + 1) * D_CHUNK].reshape(D_CHUNK * PAD_R, LOC_S)
            o = lax.dot_general(a_blk, b_blk, (((1,), (1,)), ((), ())), preferred_element_type=F32).astype(BF16)
            for i in range(RB):
                for dd in range(D_CHUNK):
                    o_buf[i // 2, dd * C_H:(dd + 1) * C_H, (i % 2) * PAD_R:(i % 2 + 1) * PAD_R] = (
                        o[i * C_H:(i + 1) * C_H, dd * PAD_R:(dd + 1) * PAD_R])
            w_blk = wt_ref[:, ch * D_CHUNK * C_H:(ch + 1) * D_CHUNK * C_H]
            for p in range(RB // 2):
                r = jnp.dot(w_blk, o_buf[p], preferred_element_type=F32)
                acc[p] = r if acc[p] is None else acc[p] + r
        for i in range(RB):
            p_buf[slot + i // UR, i % UR] = acc[i // 2][:, (i % 2) * PAD_R:(i % 2 + 1) * PAD_R].T[:LOC_R]
        row_mask = mask_t[pl.ds(pl.multiple_of(d * LOC_R + rb * RB, RB), RB), :].astype(BF16)
        col_mask = mask_t[pl.ds(columns(q), LOC_R), :].astype(BF16)
        count = lax.dot_general(col_mask, row_mask, (((1,), (1,)), ((), ())), preferred_element_type=F32)
        inv = 1.0 / (1e-3 + count)
        for u in range(UPB):
            inv_buf[slot + u] = inv[:, u * UR:(u + 1) * UR]

    def right_copy(t, peer):
        slot = lax.rem(t, S_SLOTS)
        return pltpu.make_async_remote_copy(
            src_ref=to_right.at[slot], dst_ref=from_left.at[lax.rem(t, R_SLOTS)],
            send_sem=r_send.at[slot], recv_sem=r_recv.at[lax.rem(t, R_SLOTS)],
            device_id=dev(peer, d), device_id_type=MESH)

    def left_copy(t, peer):
        slot = lax.rem(t, S_SLOTS)
        return pltpu.make_async_remote_copy(
            src_ref=to_left.at[slot], dst_ref=from_right.at[lax.rem(t, R_SLOTS)],
            send_sem=l_send.at[slot], recv_sem=l_recv.at[lax.rem(t, R_SLOTS)],
            device_id=dev(peer, d), device_id_type=MESH)

    def z_fetch(b):
        q, rb = block_of(b)
        slot = lax.rem(b, 2)
        return pltpu.make_async_copy(
            z_hbm.at[pl.ds(pl.multiple_of(rb * RB, RB), RB), pl.ds(columns(q), LOC_R), :],
            z_in.at[slot], zi_sem.at[slot])

    lag_right = z * LAG
    lag_left = (NZ - 1 - z) * LAG
    lag_end = jnp.maximum(lag_right, lag_left)

    z_fetch(0).start()
    compute(0)
    b_far.start()
    b_sib.start()
    for cp in m_copies:
        cp.start()
    m_own.start()

    def step(n, carry):
        tr = n - lag_right
        right_on = jnp.logical_and(tr >= 0, tr < N_UNITS)
        tl = n - lag_left
        left_on = jnp.logical_and(tl >= 0, tl < N_UNITS)
        send_right = jnp.logical_and(right_on, z < NZ - 1)
        send_left = jnp.logical_and(left_on, z > 0)

        @pl.when(jnp.logical_and(right_on, z > 0))
        def _():
            right_copy(tr, z - 1).wait_recv()

        @pl.when(jnp.logical_and(left_on, z < NZ - 1))
        def _():
            left_copy(tl, z + 1).wait_recv()

        @pl.when(jnp.logical_and(send_right, tr >= S_SLOTS))
        def _():
            right_copy(tr - S_SLOTS, z + 1).wait_send()

        @pl.when(jnp.logical_and(send_left, tl >= S_SLOTS))
        def _():
            left_copy(tl - S_SLOTS, z - 1).wait_send()

        @pl.when(jnp.logical_and(send_right, z == 0))
        def _():
            to_right[lax.rem(tr, S_SLOTS)] = p_buf[lax.rem(tr, P_SLOTS)].astype(BF16)

        @pl.when(jnp.logical_and(send_right, z > 0))
        def _():
            to_right[lax.rem(tr, S_SLOTS)] = (
                p_buf[lax.rem(tr, P_SLOTS)] + from_left[lax.rem(tr, R_SLOTS)].astype(F32)).astype(BF16)

        @pl.when(jnp.logical_and(send_left, z == NZ - 1))
        def _():
            to_left[lax.rem(tl, S_SLOTS)] = p_buf[lax.rem(tl, P_SLOTS)].astype(BF16)

        @pl.when(jnp.logical_and(send_left, z < NZ - 1))
        def _():
            to_left[lax.rem(tl, S_SLOTS)] = (
                p_buf[lax.rem(tl, P_SLOTS)] + from_right[lax.rem(tl, R_SLOTS)].astype(F32)).astype(BF16)

        @pl.when(send_right)
        def _():
            right_copy(tr, z + 1).start()

        @pl.when(send_left)
        def _():
            left_copy(tl, z - 1).start()

        te = n - lag_end

        @pl.when(jnp.logical_and(te >= 0, te < N_UNITS))
        def _():
            blk = lax.div(te, UPB)
            u = lax.rem(te, UPB)
            q, rb = block_of(blk)

            @pl.when(u == 0)
            def _():
                z_fetch(blk).wait()

                @pl.when(blk < N_BLOCKS - 1)
                def _():
                    z_fetch(blk + 1).start()

            p_slot = lax.rem(te, P_SLOTS)
            r_slot = lax.rem(te, R_SLOTS)
            row0 = rb * RB + u * UR

            def finish(i, total):
                inv = inv_buf[p_slot][:, i:i + 1]
                zo_ref[row0 + i, pl.ds(columns(q), LOC_R), :] = (
                    z_in[lax.rem(blk, 2), u * UR + i] + (total + bo) * inv)

            @pl.when(z == 0)
            def _():
                for i in range(UR):
                    finish(i, p_buf[p_slot, i] + from_right[r_slot, i].astype(F32))

            @pl.when(z == NZ - 1)
            def _():
                for i in range(UR):
                    finish(i, p_buf[p_slot, i] + from_left[r_slot, i].astype(F32))

            @pl.when(jnp.logical_and(z > 0, z < NZ - 1))
            def _():
                for i in range(UR):
                    finish(i, p_buf[p_slot, i] + from_left[r_slot, i].astype(F32) + from_right[r_slot, i].astype(F32))

        @pl.when(lax.rem(n, UPB) == 0)
        def _():
            nb = lax.div(n, UPB) + 1

            @pl.when(nb == N_RB)
            def _():
                b_sib.wait_recv()

            @pl.when(nb == N_RB + 2)
            def _():
                b_far.wait_recv()
                b_relay.start()

            @pl.when(nb == 3 * N_RB)
            def _():
                b_relay.wait_recv()

            @pl.when(nb < N_BLOCKS)
            def _():
                compute(nb)

        return carry

    lax.fori_loop(0, N_STEPS, step, 0)

    @pl.when(z < NZ - 1)
    def _():
        for k in range(S_SLOTS):
            right_copy(N_UNITS - S_SLOTS + k, z + 1).wait_send()

    @pl.when(z > 0)
    def _():
        for k in range(S_SLOTS):
            left_copy(N_UNITS - S_SLOTS + k, z - 1).wait_send()

    b_sib.wait_send()
    b_far.wait_send()
    b_relay.wait_send()
    m_own.wait()
    for cp in m_copies:
        cp.wait()


def combine(m, mask, gamma, beta, b_left, b_right, b_out, w_left, w_right, w_out, pair):
    any_spec = pl.BlockSpec(memory_space=pl.ANY)
    vmem_spec = pl.BlockSpec(memory_space=pltpu.VMEM)
    dma = pltpu.SemaphoreType.DMA
    return pl.pallas_call(
        main_kernel,
        in_specs=[any_spec, any_spec] + [vmem_spec] * 8 + [any_spec],
        out_specs=[vmem_spec, vmem_spec],
        out_shape=[
            pltpu.VMEM((LOC_R, N_RES, C_Z), F32),
            pltpu.VMEM((LOC_S // 4, N_RES, C_M), BF16),
        ],
        scratch_shapes=[
            pltpu.VMEM((N_Q, C_H, PAD_R, LOC_S), BF16),
            pltpu.VMEM((LOC_R * C_H, LOC_S), BF16),
            pltpu.VMEM((RB // 2, D_CHUNK * C_H, 2 * PAD_R), BF16),
            pltpu.VMEM((P_SLOTS, UR, LOC_R, C_Z), F32),
            pltpu.VMEM((P_SLOTS, LOC_R, UR), F32),
            pltpu.VMEM((R_SLOTS, UR, LOC_R, C_Z), BF16),
            pltpu.VMEM((R_SLOTS, UR, LOC_R, C_Z), BF16),
            pltpu.VMEM((S_SLOTS, UR, LOC_R, C_Z), BF16),
            pltpu.VMEM((S_SLOTS, UR, LOC_R, C_Z), BF16),
            pltpu.VMEM((2, RB, LOC_R, C_Z), F32),
            pltpu.VMEM((2, 128, N_RES), jnp.int32),
            pltpu.VMEM((N_RES, N_SEQ), F32),
            pltpu.VMEM((2, HALF_S, PRO_R, C_M), BF16),
            pltpu.VMEM((PRO_R * (PITCH + 1), 128), F32),
            pltpu.VMEM((PRO_R, C_H, LOC_S), F32),
            pltpu.VMEM((2 * C_H, C_M), BF16),
            pltpu.VMEM((C_Z, C_H * C_H), BF16),
            pltpu.VMEM((2 * C_H, 1), F32),
            dma((4,)), dma((4,)), dma((3,)), dma((3,)), dma,
            dma((S_SLOTS,)), dma((R_SLOTS,)), dma((S_SLOTS,)), dma((R_SLOTS,)), dma((2,)), dma((2,)), dma((2,)),
        ],
        compiler_params=pltpu.CompilerParams(
            collective_id=0, has_side_effects=True, vmem_limit_bytes=28 * 2**20),
        name="combine",
    )(m, mask, gamma, beta, b_left, b_right, b_out, w_left, w_right, w_out, pair)


def emit_kernel(z_ref, m_ref, zo_hbm, mo_hbm, sems):
    copies = []
    for k in range(8):
        zr = pl.ds(k * (LOC_R // 8), LOC_R // 8)
        mr = pl.ds(k * (LOC_S // 32), LOC_S // 32)
        copies.append(pltpu.make_async_copy(z_ref.at[zr], zo_hbm.at[zr], sems.at[k]))
        copies.append(pltpu.make_async_copy(m_ref.at[mr], mo_hbm.at[mr], sems.at[8 + k]))
    for cp in copies:
        cp.start()
    for cp in copies:
        cp.wait()


def emit(pair, msa):
    any_spec = pl.BlockSpec(memory_space=pl.ANY)
    vmem_spec = pl.BlockSpec(memory_space=pltpu.VMEM)
    pair = pltpu.with_memory_space_constraint(pair, pltpu.VMEM)
    msa = pltpu.with_memory_space_constraint(msa, pltpu.VMEM)
    return pl.pallas_call(
        emit_kernel,
        in_specs=[vmem_spec, vmem_spec],
        out_specs=[any_spec, any_spec],
        out_shape=[
            jax.ShapeDtypeStruct((LOC_R, N_RES, C_Z), F32),
            jax.ShapeDtypeStruct((LOC_S // 4, N_RES, C_M), BF16),
        ],
        scratch_shapes=[pltpu.SemaphoreType.DMA((16,))],
        compiler_params=pltpu.CompilerParams(vmem_limit_bytes=28 * 2**20),
        name="emit",
    )(pair, msa)


def solution(mesh):
    rep = P()
    in_specs = (P(('data', 'seq'), 'dap', None), P('data', None), P(('data', 'dap'), None, None)) + (rep,) * 8
    out_specs = (P(('data', 'dap'), None, None), P(('data', 'seq', 'dap'), None, None))

    def local_fn(m, mask, pair, ln_gamma, ln_beta, w_left, b_left, w_right, b_right, w_out, b_out):
        pair_out, msa_out = combine(m, mask, ln_gamma, ln_beta, b_left, b_right, b_out,
                                    w_left.T, w_right.T, w_out, pair)
        pair_out, msa_out = emit(pair_out, msa_out)
        return pair_out, msa_out

    return jax.shard_map(local_fn, mesh=mesh, in_specs=in_specs, out_specs=out_specs, check_vma=False)
```

time: 1370 us -> 260 us (0.19)
  waiting for transfers between devices: 719 us -> 0 us
  matrix products: 426 us -> 0 us
  Pallas kernels: 0 us -> 259 us
  local copies, waits for them, and re-layouts: 119 us -> 0 us
  other arithmetic: 84 us -> 0 us
    dot_general x27 -> x0, matrix products: 426 us -> none  [the longest x12 271 us: one_block(): jnp.einsum('icjd,cde->ije', outer_blk, w_out3, preferred_element_type=jnp...]
    psum x1 -> x0, waiting for transfers between devices: 324 us -> none  [local_fn(): summed = lax.psum(summed, 'seq')]
    pallas_call x0 -> x2, Pallas kernels: none -> 259 us  [the longest x1 249 us: combine(): pl.pallas_call(main_kernel, in_specs=[any_spec, any_spec] + [vmem_spec] *...]
    reduce_scatter x1 -> x0, waiting for transfers between devices: 258 us -> none  [local_fn(): summed = lax.psum_scatter(partial, 'dap', scatter_dimension=0, tiled=True)]
    all_to_all x1 -> x0, waiting for transfers between devices: 137 us -> none  [local_fn(): local_c7 = lax.all_to_all(array_b7, 'dap', 0, 1, tiled=True)]
    another operation x12 -> x0, local copies, waits for them, and re-layouts: 71.1 us -> none
    convert_element_type x9 -> x0, other arithmetic: 23.8 us -> none  [the longest x1 13.3 us: layer_norm(): (normed * ln_gamma.astype(jnp.float32) + ln_beta.astype(jnp.float32)).ast...]
    add x1 -> x0, other arithmetic: 20.2 us -> none  [local_fn(): return (pair_rows + update, local_c7)]
  transfers between devices with their start and end apart: 3 -> 0, of which waited for: 3 -> 0; matrix products, arithmetic and copies ran while one was open for 0% -> 0% of each run, Pallas kernels for 0% -> 0%
where the time goes in v2:
time: 260 us
  Pallas kernels  259 us (100%)
    pallas_call x1, Pallas kernels, combine(): pl.pallas_call(main_kernel, in_specs=[any_spec, any_spec] + [vmem_spec] *...  249 us
    pallas_call x1, Pallas kernels, emit(): pl.pallas_call(emit_kernel, in_specs=[vmem_spec, vmem_spec], out_specs=[a...  10.4 us

profile of v2, /device:TPU:0, one launch (start us, length us, event | category | flops | bytes accessed | tf_op | source)
XLA Modules:
  0.0 259.8 jit_solution(16557208336734172113)
XLA Ops:
  0.6 248.7 %combine.1 = (f32[96,384,128]{2,1,0:T(8,128)S(1)}, bf16[64,384,256]{2,1,0:T(8,128)(2,1)S(1)}) custom-call(bf16[256,96,256]{2,1,0:T(8,128)(2,1)} %m_hbm.1, s32[1024,384]{1,0:T(8,128)} %mask_hbm.1, bf16[256]{0:T(256)(128)(2,1)} %gamma_ref.1, bf16[256]{0:T(256)(128)(2,1)} %beta_ref.1, bf16[32]{0:T(256)(128)(2,1)} %bl_ref.1, bf16[32]{0:T(256)(128)(2,1)} %br_ref.1, ...), custom_call_target="tpu_custom_call" | custom-call | tf_op jit(solution)/shard_map/combine/pallas_call | solution.py:380
  249.3 10.4 %emit.1 = (f32[96,384,128]{2,1,0:T(8,128)}, bf16[64,384,256]{2,1,0:T(8,128)(2,1)}) custom-call(f32[96,384,128]{2,1,0:T(8,128)S(1)} %get-tuple-element.4.z_ref, bf16[64,384,256]{2,1,0:T(8,128)(2,1)S(1)} %get-tuple-element.5.m_ref), custom_call_target="tpu_custom_call" | custom-call | tf_op jit(solution)/shard_map/emit/pallas_call | solution.py:434

commit v3 on v2

--- a/solution.py
+++ b/solution.py
@@ -22,18 +22,19 @@
 N_RB = LOC_R // RB
 N_Q = 4
 N_BLOCKS = N_RB * N_Q
-UR = 4
+UR = 2
 UPB = RB // UR
 N_UNITS = N_BLOCKS * UPB
-LAG = 3
+LAG = 5
 N_STEPS = N_UNITS + 3 * LAG
-P_SLOTS = 16
+P_SLOTS = 24
 R_SLOTS = 16
-S_SLOTS = 6
+S_SLOTS = 8
 D_CHUNK = 8
 PRO_R = 16
 HALF_S = 128
-PRO_S = 16
+M_SLOTS = 4
+PRO_S = 64
 PITCH = 2 * LOC_S + 1
 
 
@@ -70,16 +71,19 @@
     def m_fetch(k, half):
         return pltpu.make_async_copy(
             m_hbm.at[pl.ds(half * HALF_S, HALF_S), pl.ds(pl.multiple_of(k * PRO_R, PRO_R), PRO_R), :],
-            m_buf.at[half], mb_sem.at[half])
+            m_buf.at[lax.rem(2 * k + half, M_SLOTS)], mb_sem.at[lax.rem(2 * k + half, M_SLOTS)])
+
+    def mask_rows_of(k):
+        return pl.multiple_of(lax.rem(2 * z + k, N_SEQ // 128) * 128, 128)
 
     def mask_fetch(k):
         return pltpu.make_async_copy(
-            mask_hbm.at[pl.ds(pl.multiple_of(k * 128, 128), 128)], mask_ref.at[lax.rem(k, 2)], mask_sem.at[lax.rem(k, 2)])
+            mask_hbm.at[pl.ds(mask_rows_of(k), 128)], mask_ref.at[lax.rem(k, 2)], mask_sem.at[lax.rem(k, 2)])
 
     mask_fetch(0).start()
     mask_fetch(1).start()
-    m_fetch(0, 0).start()
-    m_fetch(0, 1).start()
+    for k in range(M_SLOTS):
+        m_fetch(k // 2, k % 2).start()
 
     def eye(n):
         return (lax.broadcasted_iota(jnp.int32, (n, n), 0) == lax.broadcasted_iota(jnp.int32, (n, n), 1))
@@ -100,17 +104,16 @@
 
     b_all[:, :, LOC_R:, :] = jnp.zeros((N_Q, C_H, PAD_R - LOC_R, LOC_S), BF16)
 
-    def flip(k, carry):
+    def flip(k):
         mask_fetch(k).wait()
-        mask_t[:, pl.ds(pl.multiple_of(k * 128, 128), 128)] = mask_ref[lax.rem(k, 2)].astype(F32).T
+        mask_t[:, pl.ds(mask_rows_of(k), 128)] = mask_ref[lax.rem(k, 2)].astype(F32).T
 
         @pl.when(k < N_SEQ // 128 - 2)
         def _():
             mask_fetch(k + 2).start()
 
-        return carry
-
-    lax.fori_loop(0, N_SEQ // 128, flip, 0)
+    flip(jnp.int32(0))
+    flip(jnp.int32(1))
 
     at_end = jnp.logical_or(z == 0, z == NZ - 1)
     pl.semaphore_wait(barrier, jnp.where(at_end, 4, 5))
@@ -133,7 +136,7 @@
 
             def norm(step, c2):
                 start = pl.multiple_of(step * PRO_S, PRO_S)
-                x = m_buf[half, pl.ds(start, PRO_S)].astype(F32)
+                x = m_buf[lax.rem(2 * k + half, M_SLOTS), pl.ds(start, PRO_S)].astype(F32)
                 mean = jnp.mean(x, axis=-1, keepdims=True)
                 cent = x - mean
                 var = jnp.mean(cent * cent, axis=-1, keepdims=True)
@@ -146,9 +149,9 @@
 
             lax.fori_loop(0, HALF_S // PRO_S, norm, 0)
 
-            @pl.when(k < LOC_R // PRO_R - 1)
-            def _():
-                m_fetch(k + 1, half).start()
+            @pl.when(k < LOC_R // PRO_R - M_SLOTS // 2)
+            def _():
+                m_fetch(k + M_SLOTS // 2, half).start()
 
         mask_rows = mask_t[pl.ds(pl.multiple_of(d * LOC_R + k * PRO_R, PRO_R), PRO_R),
                            pl.ds(pl.multiple_of(z * LOC_S, LOC_S), LOC_S)]
@@ -160,6 +163,7 @@
             bs_ref[r] = t[C_H:]
         b_all[0, :, pl.ds(pl.multiple_of(k * PRO_R, PRO_R), PRO_R), :] = (
             jnp.swapaxes(bs_ref[...], 0, 1).astype(BF16))
+        flip(k + 2)
         return carry
 
     lax.fori_loop(0, LOC_R // PRO_R, project, 0)
@@ -236,8 +240,7 @@
     compute(0)
     b_far.start()
     b_sib.start()
-    for cp in m_copies:
-        cp.start()
+    m_copies[0].start()
     m_own.start()
 
     def step(n, carry):
@@ -338,10 +341,12 @@
             def _():
                 b_sib.wait_recv()
 
-            @pl.when(nb == N_RB + 2)
+            @pl.when(nb == N_RB - 2)
             def _():
                 b_far.wait_recv()
                 b_relay.start()
+                m_copies[1].start()
+                m_copies[2].start()
 
             @pl.when(nb == 3 * N_RB)
             def _():
@@ -398,17 +403,17 @@
             pltpu.VMEM((2, RB, LOC_R, C_Z), F32),
             pltpu.VMEM((2, 128, N_RES), jnp.int32),
             pltpu.VMEM((N_RES, N_SEQ), F32),
-            pltpu.VMEM((2, HALF_S, PRO_R, C_M), BF16),
+            pltpu.VMEM((M_SLOTS, HALF_S, PRO_R, C_M), BF16),
             pltpu.VMEM((PRO_R * (PITCH + 1), 128), F32),
             pltpu.VMEM((PRO_R, C_H, LOC_S), F32),
             pltpu.VMEM((2 * C_H, C_M), BF16),
             pltpu.VMEM((C_Z, C_H * C_H), BF16),
             pltpu.VMEM((2 * C_H, 1), F32),
             dma((4,)), dma((4,)), dma((3,)), dma((3,)), dma,
-            dma((S_SLOTS,)), dma((R_SLOTS,)), dma((S_SLOTS,)), dma((R_SLOTS,)), dma((2,)), dma((2,)), dma((2,)),
+            dma((S_SLOTS,)), dma((R_SLOTS,)), dma((S_SLOTS,)), dma((R_SLOTS,)), dma((2,)), dma((M_SLOTS,)), dma((2,)),
         ],
         compiler_params=pltpu.CompilerParams(
-            collective_id=0, has_side_effects=True, vmem_limit_bytes=28 * 2**20),
+            collective_id=0, has_side_effects=True, vmem_limit_bytes=30 * 2**20),
         name="combine",
     )(m, mask, gamma, beta, b_left, b_right, b_out, w_left, w_right, w_out, pair)
 
@@ -440,7 +445,7 @@
             jax.ShapeDtypeStruct((LOC_S // 4, N_RES, C_M), BF16),
         ],
         scratch_shapes=[pltpu.SemaphoreType.DMA((16,))],
-        compiler_params=pltpu.CompilerParams(vmem_limit_bytes=28 * 2**20),
+        compiler_params=pltpu.CompilerParams(vmem_limit_bytes=30 * 2**20),
         name="emit",
     )(pair, msa)
 

time: 260 us -> 247 us (0.950)
  Pallas kernels: 259 us -> 247 us
    pallas_call x1, Pallas kernels: 249 us -> 236 us  [combine(): pl.pallas_call(main_kernel, in_specs=[any_spec, any_spec] + [vmem_spec] *...]
where the time goes in v3:
time: 247 us
  Pallas kernels  247 us (100%)
    pallas_call x1, Pallas kernels, combine(): pl.pallas_call(main_kernel, in_specs=[any_spec, any_spec] + [vmem_spec] *...  236 us
    pallas_call x1, Pallas kernels, emit(): pl.pallas_call(emit_kernel, in_specs=[vmem_spec, vmem_spec], out_specs=[a...  10.4 us

profile of v3, /device:TPU:0, one launch (start us, length us, event | category | flops | bytes accessed | tf_op | source)
XLA Modules:
  0.0 247.2 jit_solution(12478255679844235213)
XLA Ops:
  0.6 236.2 %combine.1 = (f32[96,384,128]{2,1,0:T(8,128)S(1)}, bf16[64,384,256]{2,1,0:T(8,128)(2,1)S(1)}) custom-call(bf16[256,96,256]{2,1,0:T(8,128)(2,1)} %m_hbm.1, s32[1024,384]{1,0:T(8,128)} %mask_hbm.1, bf16[256]{0:T(256)(128)(2,1)} %gamma_ref.1, bf16[256]{0:T(256)(128)(2,1)} %beta_ref.1, bf16[32]{0:T(256)(128)(2,1)} %bl_ref.1, bf16[32]{0:T(256)(128)(2,1)} %br_ref.1, ...), custom_call_target="tpu_custom_call" | custom-call | tf_op jit(solution)/shard_map/combine/pallas_call | solution.py:385
  236.8 10.4 %emit.1 = (f32[96,384,128]{2,1,0:T(8,128)}, bf16[64,384,256]{2,1,0:T(8,128)(2,1)}) custom-call(f32[96,384,128]{2,1,0:T(8,128)S(1)} %get-tuple-element.4.z_ref, bf16[64,384,256]{2,1,0:T(8,128)(2,1)S(1)} %get-tuple-element.5.m_ref), custom_call_target="tpu_custom_call" | custom-call | tf_op jit(solution)/shard_map/emit/pallas_call | solution.py:439

commit v4 on v3

--- a/solution.py
+++ b/solution.py
@@ -25,7 +25,7 @@
 UR = 2
 UPB = RB // UR
 N_UNITS = N_BLOCKS * UPB
-LAG = 5
+LAG = 4
 N_STEPS = N_UNITS + 3 * LAG
 P_SLOTS = 24
 R_SLOTS = 16
@@ -40,7 +40,7 @@
 
 def main_kernel(m_hbm, mask_hbm, gamma_ref, beta_ref, bl_ref, br_ref, bo_ref, wl_ref, wr_ref, wo_ref, z_hbm,
                 zo_ref, mo_ref,
-                b_all, at_ref, o_buf, p_buf, inv_buf, from_left, from_right, to_right, to_left, z_in,
+                b_all, at_ref, o_buf, r_acc, p_buf, inv_buf, from_left, from_right, to_right, to_left, z_in,
                 mask_ref, mask_t, m_buf, xs_ref, bs_ref, wp_ref, wt_ref, bias_ref,
                 b_send, b_recv, m_send, m_recv, m_local,
                 r_send, r_recv, l_send, l_recv, zi_sem, mb_sem, mask_sem):
@@ -186,30 +186,30 @@
     def block_of(b):
         return lax.div(b, N_RB), lax.rem(b, N_RB)
 
-    def compute(b):
+    def compute(b, ch):
         q, rb = block_of(b)
-        slot = lax.rem(b, P_SLOTS // UPB) * UPB
         a_blk = at_ref[pl.ds(pl.multiple_of(rb * RB * C_H, RB * C_H), RB * C_H), :]
-        acc = [None] * (RB // 2)
-        for ch in range(C_H // D_CHUNK):
-            b_blk = b_all[q, ch * D_CHUNK:(ch + 1) * D_CHUNK].reshape(D_CHUNK * PAD_R, LOC_S)
-            o = lax.dot_general(a_blk, b_blk, (((1,), (1,)), ((), ())), preferred_element_type=F32).astype(BF16)
+        b_blk = b_all[q, pl.ds(ch * D_CHUNK, D_CHUNK)].reshape(D_CHUNK * PAD_R, LOC_S)
+        o = lax.dot_general(a_blk, b_blk, (((1,), (1,)), ((), ())), preferred_element_type=F32).astype(BF16)
+        for i in range(RB):
+            for dd in range(D_CHUNK):
+                o_buf[i // 2, dd * C_H:(dd + 1) * C_H, (i % 2) * PAD_R:(i % 2 + 1) * PAD_R] = (
+                    o[i * C_H:(i + 1) * C_H, dd * PAD_R:(dd + 1) * PAD_R])
+        w_blk = wt_ref[:, pl.ds(pl.multiple_of(ch * D_CHUNK * C_H, D_CHUNK * C_H), D_CHUNK * C_H)]
+        for p in range(RB // 2):
+            r_acc[p] = jnp.where(ch == 0, 0.0, r_acc[p]) + jnp.dot(w_blk, o_buf[p], preferred_element_type=F32)
+
+        @pl.when(ch == C_H // D_CHUNK - 1)
+        def _():
+            slot = lax.rem(b, P_SLOTS // UPB) * UPB
             for i in range(RB):
-                for dd in range(D_CHUNK):
-                    o_buf[i // 2, dd * C_H:(dd + 1) * C_H, (i % 2) * PAD_R:(i % 2 + 1) * PAD_R] = (
-                        o[i * C_H:(i + 1) * C_H, dd * PAD_R:(dd + 1) * PAD_R])
-            w_blk = wt_ref[:, ch * D_CHUNK * C_H:(ch + 1) * D_CHUNK * C_H]
-            for p in range(RB // 2):
-                r = jnp.dot(w_blk, o_buf[p], preferred_element_type=F32)
-                acc[p] = r if acc[p] is None else acc[p] + r
-        for i in range(RB):
-            p_buf[slot + i // UR, i % UR] = acc[i // 2][:, (i % 2) * PAD_R:(i % 2 + 1) * PAD_R].T[:LOC_R]
-        row_mask = mask_t[pl.ds(pl.multiple_of(d * LOC_R + rb * RB, RB), RB), :].astype(BF16)
-        col_mask = mask_t[pl.ds(columns(q), LOC_R), :].astype(BF16)
-        count = lax.dot_general(col_mask, row_mask, (((1,), (1,)), ((), ())), preferred_element_type=F32)
-        inv = 1.0 / (1e-3 + count)
-        for u in range(UPB):
-            inv_buf[slot + u] = inv[:, u * UR:(u + 1) * UR]
+                p_buf[slot + i // UR, i % UR] = r_acc[i // 2, :, (i % 2) * PAD_R:(i % 2 + 1) * PAD_R].T[:LOC_R]
+            row_mask = mask_t[pl.ds(pl.multiple_of(d * LOC_R + rb * RB, RB), RB), :].astype(BF16)
+            col_mask = mask_t[pl.ds(columns(q), LOC_R), :].astype(BF16)
+            count = lax.dot_general(col_mask, row_mask, (((1,), (1,)), ((), ())), preferred_element_type=F32)
+            inv = 1.0 / (1e-3 + count)
+            for u in range(UPB):
+                inv_buf[slot + u] = inv[:, u * UR:(u + 1) * UR]
 
     def right_copy(t, peer):
         slot = lax.rem(t, S_SLOTS)
@@ -237,7 +237,13 @@
     lag_end = jnp.maximum(lag_right, lag_left)
 
     z_fetch(0).start()
-    compute(0)
+    r_acc[...] = jnp.zeros(r_acc.shape, F32)
+
+    def first_block(ch, carry):
+        compute(jnp.int32(0), ch)
+        return carry
+
+    lax.fori_loop(0, UPB, first_block, 0)
     b_far.start()
     b_sib.start()
     m_copies[0].start()
@@ -333,9 +339,10 @@
                 for i in range(UR):
                     finish(i, p_buf[p_slot, i] + from_left[r_slot, i].astype(F32) + from_right[r_slot, i].astype(F32))
 
+        nb = lax.div(n, UPB) + 1
+
         @pl.when(lax.rem(n, UPB) == 0)
         def _():
-            nb = lax.div(n, UPB) + 1
 
             @pl.when(nb == N_RB)
             def _():
@@ -352,9 +359,9 @@
             def _():
                 b_relay.wait_recv()
 
-            @pl.when(nb < N_BLOCKS)
-            def _():
-                compute(nb)
+        @pl.when(nb < N_BLOCKS)
+        def _():
+            compute(nb, lax.rem(n, UPB))
 
         return carry
 
@@ -394,6 +401,7 @@
             pltpu.VMEM((N_Q, C_H, PAD_R, LOC_S), BF16),
             pltpu.VMEM((LOC_R * C_H, LOC_S), BF16),
             pltpu.VMEM((RB // 2, D_CHUNK * C_H, 2 * PAD_R), BF16),
+            pltpu.VMEM((RB // 2, C_Z, 2 * PAD_R), F32),
             pltpu.VMEM((P_SLOTS, UR, LOC_R, C_Z), F32),
             pltpu.VMEM((P_SLOTS, LOC_R, UR), F32),
             pltpu.VMEM((R_SLOTS, UR, LOC_R, C_Z), BF16),

time: 247 us -> 246 us (level)
  no operation moved by 1% of the time
where the time goes in v4:
time: 246 us
  Pallas kernels  246 us (100%)
    pallas_call x1, Pallas kernels, combine(): pl.pallas_call(main_kernel, in_specs=[any_spec, any_spec] + [vmem_spec] *...  235 us
    pallas_call x1, Pallas kernels, emit(): pl.pallas_call(emit_kernel, in_specs=[vmem_spec, vmem_spec], out_specs=[a...  10.4 us

profile of v4, /device:TPU:0, one launch (start us, length us, event | category | flops | bytes accessed | tf_op | source)
XLA Modules:
  0.0 246.2 jit_solution(13749413909017438058)
XLA Ops:
  0.6 235.1 %combine.1 = (f32[96,384,128]{2,1,0:T(8,128)S(1)}, bf16[64,384,256]{2,1,0:T(8,128)(2,1)S(1)}) custom-call(bf16[256,96,256]{2,1,0:T(8,128)(2,1)} %m_hbm.1, s32[1024,384]{1,0:T(8,128)} %mask_hbm.1, bf16[256]{0:T(256)(128)(2,1)} %gamma_ref.1, bf16[256]{0:T(256)(128)(2,1)} %beta_ref.1, bf16[32]{0:T(256)(128)(2,1)} %bl_ref.1, bf16[32]{0:T(256)(128)(2,1)} %br_ref.1, ...), custom_call_target="tpu_custom_call" | custom-call | tf_op jit(solution)/shard_map/combine/pallas_call | solution.py:392
  235.8 10.4 %emit.1 = (f32[96,384,128]{2,1,0:T(8,128)}, bf16[64,384,256]{2,1,0:T(8,128)(2,1)}) custom-call(f32[96,384,128]{2,1,0:T(8,128)S(1)} %get-tuple-element.4.z_ref, bf16[64,384,256]{2,1,0:T(8,128)(2,1)S(1)} %get-tuple-element.5.m_ref), custom_call_target="tpu_custom_call" | custom-call | tf_op jit(solution)/shard_map/emit/pallas_call | solution.py:447
